TPU v7x, 8 devices: a whole 2x2x1 slice. The times are simulated.
8 devices in a mesh: dp: 1 (over z), tp: 8 (over y, x, core).
Axes of the slice: x: 2, y: 2, z: 1, core: 2. Of those that a mesh axis runs over, the one named last changes fastest.
Arguments:
- hidden_in: bfloat16 [12, 768, 1024], P('dp', 'tp')
- ln1_gain: bfloat16 [1024], replicated
- ln1_bias: bfloat16 [1024], replicated
- w_q: bfloat16 [1024, 1024], P(None, 'tp')
- b_q: bfloat16 [1024], P('tp')
- w_k: bfloat16 [1024, 1024], P(None, 'tp')
- w_v: bfloat16 [1024, 1024], P(None, 'tp')
- b_v: bfloat16 [1024], P('tp')
- w_o: bfloat16 [1024, 1024], P('tp')
- b_o: bfloat16 [1024], replicated
- ln2_gain: bfloat16 [1024], replicated
- ln2_bias: bfloat16 [1024], replicated
- w_fc1: bfloat16 [1024, 4096], P(None, 'tp')
- b_fc1: bfloat16 [4096], P('tp')
- w_fc2: bfloat16 [4096, 1024], P('tp')
- b_fc2: bfloat16 [1024], replicated
- post_gain: bfloat16 [1024], replicated
- post_bias: bfloat16 [1024], replicated
- w_ck: bfloat16 [2, 1024, 1024], P(None, None, 'tp')
- w_cv: bfloat16 [2, 1024, 1024], P(None, None, 'tp')
- b_cv: bfloat16 [2, 1024], P(None, 'tp')
Outputs:
- output 1: bfloat16 [12, 768, 1024], P('dp', 'tp')
- output 2: bfloat16 [2, 12, 768, 16, 64], P(None, 'dp', None, 'tp')
- output 3: bfloat16 [2, 12, 768, 16, 64], P(None, 'dp', None, 'tp')
All inputs are finite; a program needn't handle non-finite values.
Results may differ from a plain program's by a relative error of at most 0.0160126.
Values are sent between devices in bfloat16 or wider.
A program may use at most 1 GiB of HBM per device.

v0:
```python
import jax
import jax.numpy as jnp
from jax import lax
from jax.sharding import PartitionSpec as P

HEAD_DIM = 64
ATTN_SCALE = HEAD_DIM ** -0.25
LN_EPS = 1e-5


def layer_norm(values, ln_gain, ln_bias):
    centered = values.astype(jnp.float32)
    centered = centered - jnp.mean(centered, axis=-1, keepdims=True)
    row_var = jnp.mean(centered * centered, axis=-1, keepdims=True)
    normed = centered * lax.rsqrt(row_var + LN_EPS)
    return (normed * ln_gain.astype(jnp.float32) + ln_bias.astype(jnp.float32)).astype(jnp.bfloat16)


def device_body(hidden_loc, ln1_gain, ln1_bias, w_q, b_q, w_k, w_v, b_v, w_o, b_o, ln2_gain, ln2_bias, w_fc1, b_fc1, w_fc2, b_fc2, post_gain, post_bias, w_ck, w_cv, b_cv):
    model_width = hidden_loc.shape[2]
    local_heads = w_q.shape[1] // HEAD_DIM
    num_layers = w_ck.shape[0]
    head_shape = (model_width, local_heads, HEAD_DIM)
    normed1 = layer_norm(hidden_loc, ln1_gain, ln1_bias)
    normed1_all = lax.all_gather(normed1, "tp", axis=1, tiled=True)
    bias_q = b_q.astype(jnp.float32).reshape(local_heads, 1, HEAD_DIM)
    bias_v = b_v.astype(jnp.float32).reshape(local_heads, 1, HEAD_DIM)
    q_heads = ((jnp.einsum("bfd,dhe->bhfe", normed1_all, w_q.reshape(head_shape), preferred_element_type=jnp.float32) + bias_q) * ATTN_SCALE).astype(jnp.bfloat16)
    k_heads = (jnp.einsum("bfd,dhe->bhfe", normed1_all, w_k.reshape(head_shape), preferred_element_type=jnp.float32) * ATTN_SCALE).astype(jnp.bfloat16)
    v_heads = (jnp.einsum("bfd,dhe->bhfe", normed1_all, w_v.reshape(head_shape), preferred_element_type=jnp.float32) + bias_v).astype(jnp.bfloat16)
    scores = jnp.einsum("bhqe,bhke->bhqk", q_heads, k_heads, preferred_element_type=jnp.float32)
    attn_probs = jax.nn.softmax(scores, axis=-1).astype(jnp.bfloat16)
    attn_heads = jnp.einsum("bhqk,bhke->bhqe", attn_probs, v_heads, preferred_element_type=jnp.float32).astype(jnp.bfloat16)
    part_attn = jnp.einsum("bhfe,hed->bfd", attn_heads, w_o.reshape(local_heads, HEAD_DIM, model_width), preferred_element_type=jnp.float32).astype(jnp.bfloat16)
    attn_sum = lax.psum_scatter(part_attn, "tp", scatter_dimension=1, tiled=True)
    attn_out = (attn_sum.astype(jnp.float32) + b_o.astype(jnp.float32)).astype(jnp.bfloat16)
    resid_one = (hidden_loc.astype(jnp.float32) + attn_out.astype(jnp.float32)).astype(jnp.bfloat16)
    normed2 = layer_norm(resid_one, ln2_gain, ln2_bias)
    normed2_all = lax.all_gather(normed2, "tp", axis=1, tiled=True)
    hidden_act = jax.nn.gelu(jnp.einsum("bfd,dc->bfc", normed2_all, w_fc1, preferred_element_type=jnp.float32) + b_fc1.astype(jnp.float32), approximate=False).astype(jnp.bfloat16)
    part_mlp = jnp.einsum("bfc,cd->bfd", hidden_act, w_fc2, preferred_element_type=jnp.float32).astype(jnp.bfloat16)
    mlp_sum = lax.psum_scatter(part_mlp, "tp", scatter_dimension=1, tiled=True)
    mlp_out = (mlp_sum.astype(jnp.float32) + b_fc2.astype(jnp.float32)).astype(jnp.bfloat16)
    resid_two = (resid_one.astype(jnp.float32) + mlp_out.astype(jnp.float32)).astype(jnp.bfloat16)
    enc_loc = layer_norm(resid_two, post_gain, post_bias)
    enc_all = lax.all_gather(enc_loc, "tp", axis=1, tiled=True)
    cache_shape = (num_layers, enc_all.shape[0], enc_all.shape[1], local_heads, HEAD_DIM)
    k_cache = jnp.einsum("bfd,ldc->lbfc", enc_all, w_ck, preferred_element_type=jnp.float32).astype(jnp.bfloat16).reshape(cache_shape)
    v_cache = (jnp.einsum("bfd,ldc->lbfc", enc_all, w_cv, preferred_element_type=jnp.float32) + b_cv.astype(jnp.float32)[:, None, None, :]).astype(jnp.bfloat16).reshape(cache_shape)
    return enc_loc, k_cache, v_cache


def solution(mesh):
    in_specs = (P("dp", "tp", None), P(), P(), P(None, "tp"), P("tp"), P(None, "tp"), P(None, "tp"), P("tp"), P("tp", None), P(), P(), P(), P(None, "tp"), P("tp"), P("tp", None), P(), P(), P(), P(None, None, "tp"), P(None, None, "tp"), P(None, "tp"))
    out_specs = (P("dp", "tp", None), P(None, "dp", None, "tp", None), P(None, "dp", None, "tp", None))
    return jax.shard_map(device_body, mesh=mesh, in_specs=in_specs, out_specs=out_specs, check_vma=False)
```

profile of v0, /device:TPU:0, one launch (start us, length us, event | category | flops | bytes accessed | tf_op | source)
XLA Modules:
  0.0 739.4 jit_solution(12388333698037593953)
XLA Ops:
  7.2 2.1 convert_reduce_fusion.1
  9.4 2.4 fusion.68
  11.8 0.7 convert_element_type.122
  12.5 0.7 convert_element_type.123
  13.2 4.0 fusion.71
  17.3 1.8 copy.36
  19.1 1.8 copy.35
  20.9 0.7 reshape.80
  21.6 1.8 copy.37
  23.4 0.7 reshape.81
  24.1 89.1 %all-gather.4.cloned.1.call-done = bf16[12,768,1024]{2,1,0:T(8,128)(2,1)} async-done(((bf16[12,96,1024]{2,1,0:T(8,128)(2,1)}), bf16[12,768,1024]{2,1,0:T(8,128)(2,1)}) %all-gather.4.cloned.1.call-update) | async-done | bytes 18874384 | tf_op jit(solution)/shard_map/all_gather | solution.py:25
  113.2 12.9 %fusion.86 = bf16[12,2,768,64]{2,3,1,0:T(8,128)(2,1)S(1)} fusion(bf16[1024,2,64,1]{0,2,1,3:T(8,128)(2,1)} %bitcast.82, bf16[12,768,1024]{2,1,0:T(8,128)(2,1)} %all-gather.4.cloned.1.call-done), kind=kOutput, calls=%fused_computation.111 | convolution fusion | flops 2418278400 | bytes 21495808 | tf_op jit(solution)/shard_map/bfd,dhe->bhfe/dot_general | solution.py:29
  126.1 7.8 %fusion.85 = bf16[12,2,768,64]{2,3,1,0:T(8,128)(2,1)} fusion(f32[2,64]{1,0:T(2,128)S(1)} %reshape.80, bf16[1024,2,64,1]{0,2,1,3:T(8,128)(2,1)S(1)} %bitcast.81, bf16[12,768,1024]{2,1,0:T(8,128)(2,1)S(1)} %copy-done.13), kind=kOutput, calls=%fused_computation.110 | convolution fusion | flops 2419458048 | bytes 21496320 | tf_op jit(solution)/shard_map/bfd,dhe->bhfe/dot_general | solution.py:28
  133.9 23.9 %fusion.137 = (f32[12,2,768]{2,1,0:T(2,128)S(1)}, f32[12,2,768,768]{2,3,1,0:T(8,128)}) fusion(bf16[12,2,768,64]{2,3,1,0:T(8,128)(2,1)} %fusion.85, bf16[12,2,768,64]{2,3,1,0:T(8,128)(2,1)S(1)} %fusion.86), kind=kOutput, calls=%fused_computation.157 | convolution fusion | flops 1840251648 | bytes 61415424 | tf_op jit(solution)/shard_map/sub | solution.py:32
  157.8 29.9 %fusion.1 = bf16[12,2,768,64]{2,3,1,0:T(8,128)(2,1)} fusion(f32[12,2,768,768]{2,3,1,0:T(8,128)} %get-tuple-element.19, f32[12,2,768]{2,1,0:T(2,128)S(1)} %get-tuple-element.18, bf16[1024,2,64,1]{0,2,1,3:T(8,128)(2,1)} %bitcast.80, bf16[12,768,1024]{2,1,0:T(8,128)(2,1)} %all-gather.4.cloned.1.call-done, f32[2,64]{1,0:T(2,128)S(1)} %reshape.81), kind=kOutput, calls=%fused_computation.4 | convolution fusion | flops 4258529280 | bytes 78193152 | tf_op jit(solution)/shard_map/bhqk,bhke->bhqe/dot_general | solution.py:33
  187.8 11.6 %bitcast_convert_fusion = bf16[12,768,1024]{2,1,0:T(8,128)(2,1)} fusion(bf16[2,64,1024,1]{2,1,0,3:T(8,128)(2,1)} %bitcast.83, bf16[12,2,768,64]{2,3,1,0:T(8,128)(2,1)} %fusion.1), kind=kOutput, calls=%fused_computation.3 | convolution fusion | flops 2425356288 | bytes 21495808 | tf_op jit(solution)/shard_map/bhfe,hed->bfd/dot_general | solution.py:34
  199.5 117.1 %reduce-scatter.3.cloned.1.call-done = bf16[12,96,1024]{2,1,0:T(8,128)(2,1)} async-done(((bf16[12,768,1024]{2,1,0:T(8,128)(2,1)}), bf16[12,96,1024]{2,1,0:T(8,128)(2,1)}) %reduce-scatter.3.cloned.1.call-update) | async-done | bytes 2359312 | tf_op jit(solution)/shard_map/reduce_scatter | solution.py:35
  316.6 2.6 convert_reduce_fusion
  319.2 0.8 fusion.64
  320.6 2.3 fusion.67
  323.0 93.0 %all-gather.6.cloned.1.call-done = bf16[12,768,1024]{2,1,0:T(8,128)(2,1)} async-done(((bf16[12,96,1024]{2,1,0:T(8,128)(2,1)}), bf16[12,768,1024]{2,1,0:T(8,128)(2,1)}) %all-gather.6.cloned.1.call-update) | async-done | bytes 18874384 | tf_op jit(solution)/shard_map/all_gather | solution.py:39
  416.1 23.6 %fusion.57 = (u16[768,512]{1,0:T(8,128)(2,1)S(1)}, u16[768,512]{1,0:T(8,128)(2,1)S(1)}, f32[12,768,512]{2,1,0:T(8,128)}) fusion(f32[512]{0:T(512)S(1)} %convert_element_type.143, bf16[12,768,1024]{2,1,0:T(8,128)(2,1)} %all-gather.6.cloned.1.call-done, bf16[1024,512]{1,0:T(8,128)(2,1)} %param.33), kind=kOutput, calls=%fused_computation.73 | convolution fusion | flops 9728950272 | bytes 40372224 | tf_op jit(solution)/shard_map/bfd,dc->bfc/dot_general | solution.py:40
  439.7 53.4 %convolution_convert_fusion = bf16[12,768,1024]{2,1,0:T(8,128)(2,1)} fusion(f32[12,768,512]{2,1,0:T(8,128)} %get-tuple-element.20, f32[512]{0:T(512)S(1)} %convert_element_type.143, u16[768,512]{1,0:T(8,128)(2,1)S(1)} %get-tuple-element.13, u16[768,512]{1,0:T(8,128)(2,1)S(1)} %get-tuple-element.12, bf16[512,1024]{1,0:T(8,128)(2,1)S(1)} %copy-done), kind=kOutput, calls=%fused_computation.38 | convolution fusion | flops 10008133632 | bytes 40372224 | tf_op jit(solution)/shard_map/bfc,cd->bfd/dot_general | solution.py:41
  493.8 116.5 %reduce-scatter.5.cloned.1.call-done = bf16[12,96,1024]{2,1,0:T(8,128)(2,1)} async-done(((bf16[12,768,1024]{2,1,0:T(8,128)(2,1)}), bf16[12,96,1024]{2,1,0:T(8,128)(2,1)}) %reduce-scatter.5.cloned.1.call-update) | async-done | bytes 2359312 | tf_op jit(solution)/shard_map/reduce_scatter | solution.py:42
  610.3 2.6 convert_reduce_fusion.2
  612.9 0.8 fusion.72
  613.7 2.3 fusion.75
  616.1 93.1 %all-gather.8.cloned.1.call-done = bf16[12,768,1024]{2,1,0:T(8,128)(2,1)} async-done(((bf16[12,96,1024]{2,1,0:T(8,128)(2,1)}), bf16[12,768,1024]{2,1,0:T(8,128)(2,1)}) %all-gather.8.cloned.1.call-update) | async-done | bytes 18874384 | tf_op jit(solution)/shard_map/all_gather | solution.py:46
  709.2 9.3 %add_convert_fusion = bf16[12,768,2,128]{1,3,2,0:T(8,128)(2,1)S(1)} fusion(f32[2,128]{1,0:T(2,128)S(1)} %convert_element_type.157, bf16[12,768,1024]{2,1,0:T(8,128)(2,1)} %all-gather.8.cloned.1.call-done, bf16[2,1024,128]{2,1,0:T(8,128)(2,1)S(1)} %copy-done.14), kind=kOutput, calls=%fused_computation.40 | convolution fusion | flops 4836556800 | bytes 24118272 | tf_op jit(solution)/shard_map/bfd,ldc->lbfc/dot_general | solution.py:49
  718.5 2.5 copy.42
  721.0 9.1 %fusion.82 = bf16[12,768,2,128]{1,3,2,0:T(8,128)(2,1)S(1)} fusion(bf16[12,768,1024]{2,1,0:T(8,128)(2,1)} %all-gather.8.cloned.1.call-done, bf16[2,1024,128]{2,1,0:T(8,128)(2,1)S(1)} %copy-done.15), kind=kOutput, calls=%fused_computation.109 | convolution fusion | flops 4834197504 | bytes 24117248 | tf_op jit(solution)/shard_map/bfd,ldc->lbfc/dot_general | solution.py:48
  730.1 2.5 copy.41
  (58 shorter events, 1.6 us)
Async XLA Ops:
  7.2 432.5 %copy-start = (bf16[512,1024]{1,0:T(8,128)(2,1)S(1)}, bf16[512,1024]{1,0:T(8,128)(2,1)}, u32[]{:S(2)}) copy-start(bf16[512,1024]{1,0:T(8,128)(2,1)} %param.35) | copy-start | bytes 3145732
  7.2 106.0 %all-gather.4.cloned.1.call-start = ((), (), s32[]{:S(2)}) async-start(), calls=%async_computation.2 | async-start | bytes 21233664 | tf_op jit(solution)/shard_map/all_gather | solution.py:25
  17.2 299.4 %reduce-scatter.3.cloned.1.call-start = ((), (), s32[]{:S(2)}) async-start(), calls=%async_computation.3 | async-start | bytes 21233664 | tf_op jit(solution)/shard_map/reduce_scatter | solution.py:35
  113.2 12.9 %copy-start.5 = (bf16[1024,128]{0,1:T(8,128)(2,1)S(1)}, bf16[1024,128]{0,1:T(8,128)(2,1)}, u32[]{:S(2)}) copy-start(bf16[1024,128]{0,1:T(8,128)(2,1)} %copy.35) | copy-start | bytes 786436
  113.2 12.9 %copy-start.13 = (bf16[12,768,1024]{2,1,0:T(8,128)(2,1)S(1)}, bf16[12,768,1024]{2,1,0:T(8,128)(2,1)}, u32[]{:S(2)}) copy-start(bf16[12,768,1024]{2,1,0:T(8,128)(2,1)} %all-gather.4.cloned.1.call-done) | copy-start | bytes 56623108
  187.7 11.7 %copy-start.6 = (bf16[1024]{0:T(1024)(128)(2,1)S(1)}, bf16[1024]{0:T(1024)(128)(2,1)}, u32[]{:S(2)}) copy-start(bf16[1024]{0:T(1024)(128)(2,1)} %param.30) | copy-start | bytes 6148
  187.7 11.7 %copy-start.7 = (bf16[1024]{0:T(1024)(128)(2,1)S(1)}, bf16[1024]{0:T(1024)(128)(2,1)}, u32[]{:S(2)}) copy-start(bf16[1024]{0:T(1024)(128)(2,1)} %param.31) | copy-start | bytes 6148
  187.7 11.7 %copy-start.8 = (bf16[1024]{0:T(1024)(128)(2,1)S(1)}, bf16[1024]{0:T(1024)(128)(2,1)}, u32[]{:S(2)}) copy-start(bf16[1024]{0:T(1024)(128)(2,1)} %param.32) | copy-start | bytes 6148
  187.8 128.8 %copy-start.2 = (bf16[12,96,1024]{2,1,0:T(8,128)(2,1)S(1)}, bf16[12,96,1024]{2,1,0:T(8,128)(2,1)}, u32[]{:S(2)}) copy-start(bf16[12,96,1024]{2,1,0:T(8,128)(2,1)} %param.21) | copy-start | bytes 7077892
  199.3 123.6 %copy-start.12 = (bf16[512]{0:T(512)(128)(2,1)S(1)}, bf16[512]{0:T(512)(128)(2,1)}, u32[]{:S(2)}) copy-start(bf16[512]{0:T(512)(128)(2,1)} %param.34) | copy-start | bytes 3076
  199.4 216.7 %all-gather.6.cloned.1.call-start = ((), (), s32[]{:S(2)}) async-start(), calls=%async_computation.4 | async-start | bytes 21233664 | tf_op jit(solution)/shard_map/all_gather | solution.py:39
  319.2 1.4 copy-start.3
  322.9 287.4 %reduce-scatter.5.cloned.1.call-start = ((), (), s32[]{:S(2)}) async-start(), calls=%async_computation.5 | async-start | bytes 21233664 | tf_op jit(solution)/shard_map/reduce_scatter | solution.py:42
  493.1 0.7 copy-start.9
  493.1 0.7 copy-start.10
  493.1 0.7 copy-start.11
  493.1 117.3 %copy-start.4 = (bf16[12,96,1024]{2,1,0:T(8,128)(2,1)S(1)}, bf16[12,96,1024]{2,1,0:T(8,128)(2,1)}, u32[]{:S(2)}) copy-start(bf16[12,96,1024]{2,1,0:T(8,128)(2,1)} %copy-done.3) | copy-start | bytes 7077892
  493.1 123.0 %copy-start.16 = (bf16[2,128]{1,0:T(2,128)(2,1)S(1)}, bf16[2,128]{1,0:T(2,128)(2,1)}, u32[]{:S(2)}) copy-start(bf16[2,128]{1,0:T(2,128)(2,1)} %param.41) | copy-start | bytes 1540
  493.1 216.1 %copy-start.14 = (bf16[2,1024,128]{2,1,0:T(8,128)(2,1)S(1)}, bf16[2,1024,128]{2,1,0:T(8,128)(2,1)}, u32[]{:S(2)}) copy-start(bf16[2,1024,128]{2,1,0:T(8,128)(2,1)} %param.40) | copy-start | bytes 1572868
  493.1 216.1 %all-gather.8.cloned.1.call-start = ((), (), s32[]{:S(2)}) async-start(), calls=%async_computation.6 | async-start | bytes 21233664 | tf_op jit(solution)/shard_map/all_gather | solution.py:46
  616.1 104.9 %copy-start.15 = (bf16[2,1024,128]{2,1,0:T(8,128)(2,1)S(1)}, bf16[2,1024,128]{2,1,0:T(8,128)(2,1)}, u32[]{:S(2)}) copy-start(bf16[2,1024,128]{2,1,0:T(8,128)(2,1)} %param.39) | copy-start | bytes 1572868
  718.5 14.1 %copy-start.1 = (bf16[512,1024]{1,0:T(8,128)(2,1)S(1)}, bf16[512,1024]{1,0:T(8,128)(2,1)}, u32[]{:S(2)}) copy-start(bf16[512,1024]{1,0:T(8,128)(2,1)} %param.35) | copy-start | bytes 3145732
Sparse Core Ops, SparseCore 0:
  17.3 95.8 all-gather.3
  199.5 117.0 reduce-scatter.2
  323.1 92.9 all-gather.5
  493.3 117.0 reduce-scatter.4
  616.2 92.9 all-gather.7
where the time goes:
time: 745 us; the launch traced here: 739 us
  waiting for transfers between devices  509 us (68%)
  matrix products  181 us (24%)
  other arithmetic  21.4 us (3%)
  between operations  14.3 us (2%)
  local copies, waits for them, and re-layouts  13.1 us (2%)
    reduce_scatter x1, waiting for transfers between devices, device_body(): lax.psum_scatter(part_attn, 'tp', scatter_dimension=1, tiled=True)  117 us
    reduce_scatter x1, waiting for transfers between devices, device_body(): mlp_sum = lax.psum_scatter(part_mlp, 'tp', scatter_dimension=1, tiled=True)  117 us
    all_gather x1, waiting for transfers between devices, device_body(): enc_all = lax.all_gather(enc_loc, 'tp', axis=1, tiled=True)  93.1 us
    all_gather x1, waiting for transfers between devices, device_body(): normed2_all = lax.all_gather(normed2, 'tp', axis=1, tiled=True)  93 us
    all_gather x1, waiting for transfers between devices, device_body(): normed1_all = lax.all_gather(normed1, 'tp', axis=1, tiled=True)  89.1 us
    dot_general x1, matrix products, device_body(): jnp.einsum('bfc,cd->bfd', hidden_act, w_fc2, preferred_element_type=jnp.f...  53.4 us
    dot_general x1, matrix products, device_body(): jnp.einsum('bhqk,bhke->bhqe', attn_probs, v_heads, preferred_element_type...  29.9 us
    sub x1, matrix products, device_body(): attn_probs = jax.nn.softmax(scores, axis=-1).astype(jnp.bfloat16)  23.9 us
  transfers between devices with their start and end apart: 5, of which 5 were waited for; matrix products, arithmetic and copies ran while one was open for 1% of the time, Pallas kernels for 0%

commit v1 on v0

v1 whole, which is shorter than its diff:
```python
import numpy as np
import jax
import jax.numpy as jnp
from jax import lax
from jax.sharding import PartitionSpec as P

HEAD_DIM = 64
ATTN_SCALE = HEAD_DIM ** -0.25
LN_EPS = 1e-5


def layer_norm(values, ln_gain, ln_bias):
    centered = values.astype(jnp.float32)
    centered = centered - jnp.mean(centered, axis=-1, keepdims=True)
    row_var = jnp.mean(centered * centered, axis=-1, keepdims=True)
    normed = centered * lax.rsqrt(row_var + LN_EPS)
    return (normed * ln_gain.astype(jnp.float32) + ln_bias.astype(jnp.float32)).astype(jnp.bfloat16)


def device_body(hidden_loc, ln1_gain, ln1_bias, w_q, b_q, w_k, w_v, b_v, w_o, b_o, ln2_gain, ln2_bias, w_fc1, b_fc1, w_fc2, b_fc2, post_gain, post_bias, w_ck, w_cv, b_cv):
    f32, bf16 = jnp.float32, jnp.bfloat16
    clips, frames, width = hidden_loc.shape
    n = lax.axis_size("tp")
    per_chip = clips // (n // 2)
    core = lax.rem(lax.axis_index("tp"), 2)
    order = [per_chip * (d // 2) + (2 * (d % 2) if j == 0 else 1) for d in range(n) for j in range(2)]
    send = jnp.stack([hidden_loc[c] for c in order]).reshape(n, 2, frames, width)
    recv = lax.all_to_all(send, "tp", split_axis=0, concat_axis=0)
    total = n * frames
    x2 = recv.transpose(1, 0, 2, 3).reshape(2, total, width)
    half = total // 2

    qkv = lax.all_gather(jnp.concatenate([w_q, w_k, w_v], axis=1), "tp", axis=0)
    wo_all = lax.all_gather(w_o, "tp", axis=0, tiled=True)
    w1_all = lax.all_gather(w_fc1, "tp", axis=0)
    w2_all = lax.all_gather(w_fc2, "tp", axis=0, tiled=True)
    bias_q = lax.all_gather(b_q, "tp", axis=0, tiled=True).astype(f32)
    bias_v = lax.all_gather(b_v, "tp", axis=0, tiled=True).astype(f32)
    bias_1 = lax.all_gather(b_fc1, "tp", axis=0, tiled=True).astype(f32)

    a2 = layer_norm(x2, ln1_gain, ln1_bias)
    a_shared = lax.dynamic_slice_in_dim(a2[1], core * half, half, 0)
    x_shared = lax.dynamic_slice_in_dim(x2[1], core * half, half, 0)
    a_own = jnp.concatenate([a2[0], a_shared]).reshape(3, half, width)
    x_own = jnp.concatenate([x2[0], x_shared]).reshape(3 * half, width)
    heads = width // HEAD_DIM
    wq = qkv[:, :, : w_q.shape[1]]
    wk = qkv[:, :, w_q.shape[1]: 2 * w_q.shape[1]]
    wv = qkv[:, :, 2 * w_q.shape[1]:]
    q = jnp.einsum("btd,ndc->btnc", a_own, wq, preferred_element_type=f32).reshape(3, half, width)
    q = ((q + bias_q) * ATTN_SCALE).astype(bf16).reshape(3, half, heads, HEAD_DIM)
    k = (jnp.einsum("btd,ndc->btnc", a2, wk, preferred_element_type=f32) * ATTN_SCALE).astype(bf16).reshape(2, total, heads, HEAD_DIM)
    v = (jnp.einsum("btd,ndc->btnc", a2, wv, preferred_element_type=f32).reshape(2, total, width) + bias_v).astype(bf16).reshape(2, total, heads, HEAD_DIM)

    def attend(qq, kk, vv):
        s = jnp.einsum("qhe,khe->hqk", qq, kk, preferred_element_type=f32)
        p = jax.nn.softmax(s, axis=-1).astype(bf16)
        return jnp.einsum("hqk,khe->qhe", p, vv, preferred_element_type=f32).astype(bf16)

    o = jnp.concatenate([attend(q[:2].reshape(total, heads, HEAD_DIM), k[0], v[0]), attend(q[2], k[1], v[1])]).reshape(3 * half, width)
    attn_out = (jnp.dot(o, wo_all, preferred_element_type=f32) + b_o.astype(f32)).astype(bf16)
    h = (x_own.astype(f32) + attn_out.astype(f32)).astype(bf16)
    m = layer_norm(h, ln2_gain, ln2_bias)
    g = jnp.einsum("td,ndc->tnc", m, w1_all, preferred_element_type=f32).reshape(3 * half, -1)
    g = jax.nn.gelu(g + bias_1, approximate=False).astype(bf16)
    mlp = (jnp.dot(g, w2_all, preferred_element_type=f32) + b_fc2.astype(f32)).astype(bf16)
    h2 = (h.astype(f32) + mlp.astype(f32)).astype(bf16)
    e = layer_norm(h2, post_gain, post_bias)
    num_layers, local = w_ck.shape[0], w_ck.shape[2]
    me = lax.axis_index("tp")
    e_parts = [lax.all_gather(e[j * half:(j + 1) * half], "tp", axis=0) for j in range(3)]
    by_clip = []
    for c in range(n // 2):
        by_clip.append(jnp.concatenate([e_parts[0][2 * c], e_parts[1][2 * c]]))
        by_clip.append(jnp.concatenate([e_parts[2][2 * c], e_parts[2][2 * c + 1]]))
        by_clip.append(jnp.concatenate([e_parts[0][2 * c + 1], e_parts[1][2 * c + 1]]))
    e_all = jnp.stack(by_clip)
    enc = lax.dynamic_slice_in_dim(e_all, me * frames, frames, 1)
    cache_shape = (num_layers, clips, total, local // HEAD_DIM, HEAD_DIM)
    k_cache = jnp.einsum("bfd,ldc->lbfc", e_all, w_ck, preferred_element_type=f32).astype(bf16).reshape(cache_shape)
    v_cache = (jnp.einsum("bfd,ldc->lbfc", e_all, w_cv, preferred_element_type=f32) + b_cv.astype(f32)[:, None, None, :]).astype(bf16).reshape(cache_shape)
    return enc, k_cache, v_cache


def solution(mesh):
    in_specs = (P("dp", "tp", None), P(), P(), P(None, "tp"), P("tp"), P(None, "tp"), P(None, "tp"), P("tp"), P("tp", None), P(), P(), P(), P(None, "tp"), P("tp"), P("tp", None), P(), P(), P(), P(None, None, "tp"), P(None, None, "tp"), P(None, "tp"))
    out_specs = (P("dp", "tp", None), P(None, "dp", None, "tp", None), P(None, "dp", None, "tp", None))
    return jax.shard_map(device_body, mesh=mesh, in_specs=in_specs, out_specs=out_specs, check_vma=False)
```

time: 745 us -> 503 us (0.68)
  waiting for transfers between devices: 509 us -> 117 us
  blocking collectives: 0 us -> 74.6 us
  local copies, waits for them, and re-layouts: 13.1 us -> 80.9 us
  other arithmetic: 21.4 us -> 85.5 us
  matrix products: 181 us -> 120 us
    reduce_scatter x2 -> x0, waiting for transfers between devices: 234 us -> none  [the longest x1 117 us: device_body(): lax.psum_scatter(part_attn, 'tp', scatter_dimension=1, tiled=True)]
    all_gather x3 -> x7, waiting for transfers between devices: 275 us -> 114 us  [the longest x3 114 us: device_body(): lax.all_gather(e[j * half:(j + 1) * half], 'tp', axis=0)]
    all_gather x0 -> x3, blocking collectives: none -> 74.6 us  [the longest x1 53.1 us: device_body(): bias_q = lax.all_gather(b_q, 'tp', axis=0, tiled=True).astype(f32)]
    dot_general x8 -> x10, matrix products: 158 us -> 102 us  [the longest x2 25.3 us: attend(): jnp.einsum('hqk,khe->qhe', p, vv, preferred_element_type=f32).astype(bf16)]
    convert_element_type x4 -> x8, other arithmetic: 0.01 us -> 50.6 us  [the longest x1 46.8 us: device_body(): g = jax.nn.gelu(g + bias_1, approximate=False).astype(bf16)]
    slice x0 -> x13, local copies, waits for them, and re-layouts: none -> 31.2 us  [the longest x2 6.35 us: device_body(): q[:2].reshape(total, heads, HEAD_DIM)]
    unnamed x39 -> x94, local copies, waits for them, and re-layouts: 11.6 us -> 23.9 us
    unnamed x0 -> x8, other arithmetic: none -> 12 us
  transfers between devices with their start and end apart: 5 -> 8, of which waited for: 5 -> 3; matrix products, arithmetic and copies ran while one was open for 1% -> 42% of each run, Pallas kernels for 0% -> 0%
where the time goes in v1:
time: 503 us; the launch traced here: 498 us
  matrix products  120 us (24%)
  waiting for transfers between devices  117 us (23%)
  other arithmetic  85.5 us (17%)
  local copies, waits for them, and re-layouts  80.9 us (16%)
  blocking collectives  74.6 us (15%)
  between operations  15.1 us (3%)
    all_gather x3, waiting for transfers between devices, device_body(): lax.all_gather(e[j * half:(j + 1) * half], 'tp', axis=0)  114 us
    all_gather x1, blocking collectives, device_body(): bias_q = lax.all_gather(b_q, 'tp', axis=0, tiled=True).astype(f32)  53.1 us
    convert_element_type x1, other arithmetic, device_body(): g = jax.nn.gelu(g + bias_1, approximate=False).astype(bf16)  46.8 us
    dot_general x2, matrix products, attend(): jnp.einsum('hqk,khe->qhe', p, vv, preferred_element_type=f32).astype(bf16)  25.3 us
    unnamed x94, local copies, waits for them, and re-layouts  23.9 us
    sub x2, matrix products, attend(): p = jax.nn.softmax(s, axis=-1).astype(bf16)  18 us
    dot_general x1, matrix products, device_body(): jnp.einsum('td,ndc->tnc', m, w1_all, preferred_element_type=f32)  17.6 us
    dot_general x1, matrix products, device_body(): jnp.dot(g, w2_all, preferred_element_type=f32) + b_fc2.astype(f32)  16.6 us
  transfers between devices with their start and end apart: 8, of which 3 were waited for; matrix products, arithmetic and copies ran while one was open for 42% of the time, Pallas kernels for 0%

profile of v1, /device:TPU:0, one launch (start us, length us, event | category | flops | bytes accessed | tf_op | source)
XLA Modules:
  0.0 498.1 jit_solution(1928379544911140961)
XLA Ops:
  14.1 4.3 all-to-all-start
  19.1 53.1 %all-gather.6 = bf16[8,1,128]{2,1,0:T(2,128)(2,1)S(1)} all-gather(bf16[1,1,128]{2,1,0:T(2,128)(2,1)S(1)} %bitcast.189), channel_id=1, replica_groups=mesh['dp'=1,'tp'=8] {'tp'}, dimensions={0}, use_global_device_ids=true | all-gather | bytes 2304 | tf_op jit(solution)/shard_map/all_gather | solution.py:37
  72.2 10.8 %all-gather.5 = bf16[8,1,128]{2,1,0:T(2,128)(2,1)S(1)} all-gather(bf16[1,1,128]{2,1,0:T(2,128)(2,1)S(1)} %bitcast.190), channel_id=1, replica_groups=mesh['dp'=1,'tp'=8] {'tp'}, dimensions={0}, use_global_device_ids=true | all-gather | bytes 2304 | tf_op jit(solution)/shard_map/all_gather | solution.py:38
  83.1 10.8 %all-gather.7 = bf16[8,1,512]{2,1,0:T(2,128)(2,1)S(1)} all-gather(bf16[1,1,512]{2,1,0:T(2,128)(2,1)S(1)} %reshape.193), channel_id=1, replica_groups=mesh['dp'=1,'tp'=8] {'tp'}, dimensions={0}, use_global_device_ids=true | all-gather | bytes 9216 | tf_op jit(solution)/shard_map/all_gather | solution.py:39
  98.8 2.9 multiply_reduce_fusion
  122.5 3.0 pad_maximum_fusion
  125.5 4.1 slice_bitcast_fusion.4
  129.6 6.5 %multiply_convert_fusion = bf16[2,768,8,128]{1,3,2,0:T(8,128)(2,1)} fusion(bf16[8,1024,384]{2,1,0:T(8,128)(2,1)} %bitcast.171, bf16[2,768,1024]{2,1,0:T(8,128)(2,1)S(1)} %copy-done.2), kind=kOutput, calls=%fused_computation.41 | convolution fusion | flops 3224371200 | bytes 8388608 | tf_op jit(solution)/shard_map/btd,ndc->btnc/dot_general | solution.py:52
  136.2 3.9 copy.134
  140.1 5.0 multiply_convert_fusion.1
  147.0 5.0 %copy.135 = bf16[2,384,1024]{1,0,2:T(2,128)(2,1)} copy(bf16[2,384,1024]{2,1,0:T(8,128)(2,1)} %slice.247) | data formatting | bytes 3145728 | tf_op jit(solution)/shard_map/slice | solution.py:60
  151.9 4.9 reshape.130
  156.8 3.8 fusion.89
  163.4 6.0 %add_convert_fusion.1 = bf16[2,768,1024]{2,1,0:T(8,128)(2,1)S(1)} fusion(f32[1024]{0:T(1024)S(1)} %bitcast.187, bf16[2,768,1024]{2,1,0:T(8,128)(2,1)} %bitcast.169, bf16[1024,1024,1]{1,0,2:T(8,128)(2,1)} %bitcast.175), kind=kOutput, calls=%fused_computation.42 | convolution fusion | flops 3224371200 | bytes 8392704 | tf_op jit(solution)/shard_map/btd,ndc->btnc/dot_general | solution.py:53
  176.1 11.0 %fusion.93 = f32[16,768]{1,0:T(8,128)S(1)} fusion(bf16[768,16,64]{0,2,1:T(8,128)(2,1)} %reshape.130, bf16[768,16,64]{0,2,1:T(8,128)(2,1)} %bitcast.180), kind=kOutput, calls=%fused_computation.143 | convolution fusion | flops 1226834688 | bytes 3194880 | tf_op jit(solution)/shard_map/sub | solution.py:57
  187.2 16.0 %fusion.69 = bf16[768,16,64]{0,2,1:T(8,128)(2,1)} fusion(bf16[768,16,64]{0,2,1:T(8,128)(2,1)} %bitcast.177, f32[16,768]{1,0:T(8,128)S(1)} %fusion.93, bf16[768,16,64]{0,2,1:T(8,128)(2,1)S(1)} %copy-done.15, bf16[768,16,64]{0,2,1:T(8,128)(2,1)} %bitcast.181), kind=kOutput, calls=%fused_computation.108 | convolution fusion | flops 2445030144 | bytes 6340608 | tf_op jit(solution)/shard_map/hqk,khe->qhe/dot_general | solution.py:58
  203.2 7.0 %fusion.92 = f32[16,384]{1,0:T(8,128)S(1)} fusion(bf16[384,16,64]{0,2,1:T(8,128)(2,1)S(1)} %bitcast.185, bf16[768,16,64]{0,2,1:T(8,128)(2,1)} %bitcast.178), kind=kOutput, calls=%fused_computation.142 | convolution fusion | flops 613417728 | bytes 2383872 | tf_op jit(solution)/shard_map/sub | solution.py:57
  210.2 9.3 %fusion.71 = bf16[384,16,64]{0,2,1:T(8,128)(2,1)S(1)} fusion(bf16[768,16,64]{0,2,1:T(8,128)(2,1)S(1)} %bitcast.176, f32[16,384]{1,0:T(8,128)S(1)} %fusion.92, bf16[384,16,64]{0,2,1:T(8,128)(2,1)} %bitcast.184, bf16[768,16,64]{0,2,1:T(8,128)(2,1)} %bitcast.179), kind=kOutput, calls=%fused_computation.110 | convolution fusion | flops 1222515456 | bytes 4743168 | tf_op jit(solution)/shard_map/hqk,khe->qhe/dot_general | solution.py:58
  219.5 3.1 pad_maximum_fusion.1
  222.6 6.1 %convert_reduce_fusion = (f32[1152]{0:T(1024)S(1)}, bf16[1152,1024]{0,1:T(8,128)(2,1)S(1)}) fusion(f32[1024]{0:T(1024)S(1)} %convert_element_type.151, bf16[1152,1024]{0,1:T(8,128)(2,1)} %bitcast.173, bf16[1024,1024]{1,0:T(8,128)(2,1)} %all-gather.16.cloned.1.call-done, bf16[384,1024]{0,1:T(8,128)(2,1)} %copy.164, bf16[768,1024]{0,1:T(8,128)(2,1)} %copy.125), kind=kOutput, calls=%fused_computation.35 | convolution fusion | flops 2428894208 | bytes 9183744 | tf_op jit(solution)/shard_map/dot_general | solution.py:61
  229.4 17.6 %fusion.46 = f32[1152,8,512]{0,2,1:T(8,128)} fusion(bf16[8,1024,512]{2,1,0:T(8,128)(2,1)} %bitcast.191, bf16[1152,1024]{0,1:T(8,128)(2,1)S(1)} %get-tuple-element.51, f32[1024]{0:T(1024)S(1)} %convert_element_type.157, f32[1024]{0:T(1024)S(1)} %convert_element_type.156, f32[1152]{0:T(1024)S(1)} %add_rsqrt_fusion.1, f32[1152]{0:T(1024)S(1)} %broadcast_multiply_fusion.1), kind=kOutput, calls=%fused_computation.71 | convolution fusion | flops 9670754304 | bytes 29639680 | tf_op jit(solution)/shard_map/td,ndc->tnc/dot_general | solution.py:64
  247.1 46.8 %fusion.4 = bf16[1152,4096]{0,1:T(8,128)(2,1)} fusion(f32[1152,8,512]{0,2,1:T(8,128)} %fusion.46, f32[4096]{0:T(1024)S(1)} %bitcast.186), kind=kLoop, calls=%fused_computation.7 | loop fusion | flops 311427072 | bytes 28327936 | tf_op jit(solution)/shard_map/convert_element_type | solution.py:65
  293.9 16.6 %convert_reduce_fusion.1 = (f32[1152]{0:T(1024)S(1)}, bf16[1152,1024]{0,1:T(8,128)(2,1)S(1)}) fusion(f32[1024]{0:T(1024)S(1)} %copy-done.21, bf16[1152,4096]{0,1:T(8,128)(2,1)} %fusion.4, bf16[4096,1024]{1,0:T(8,128)(2,1)} %all-gather.18.cloned.1.call-done, bf16[1152,1024]{0,1:T(8,128)(2,1)S(1)} %get-tuple-element.51), kind=kOutput, calls=%fused_computation.46 | convolution fusion | flops 9673112576 | bytes 22553088 | tf_op jit(solution)/shard_map/dot_general | solution.py:66
  315.0 39.5 %all-gather.24.cloned.1.call-done = bf16[3072,1024]{0,1:T(8,128)(2,1)} async-done(((bf16[384,1024]{0,1:T(8,128)(2,1)}), bf16[3072,1024]{0,1:T(8,128)(2,1)}) %all-gather.24.cloned.1.call-update) | async-done | bytes 6291472 | tf_op jit(solution)/shard_map/all_gather | solution.py:71
  354.6 5.1 %fusion.86 = (bf16[384,1024]{0,1:T(8,128)(2,1)S(1)}, bf16[384,1024]{0,1:T(8,128)(2,1)S(1)}, bf16[384,1024]{0,1:T(8,128)(2,1)S(1)}, bf16[384,1024]{0,1:T(8,128)(2...) fusion(bf16[3072,1024]{0,1:T(8,128)(2,1)} %all-gather.24.cloned, ...), kind=kLoop, calls=%fused_computation.136 | loop fusion | bytes 12582912 | tf_op jit(solution)/shard_map/slice | solution.py:76
  359.6 37.9 %all-gather.26.cloned.1.call-done = bf16[3072,1024]{0,1:T(8,128)(2,1)} async-done(((bf16[384,1024]{0,1:T(8,128)(2,1)}), bf16[3072,1024]{0,1:T(8,128)(2,1)}) %all-gather.26.cloned.1.call-update) | async-done | bytes 6291472 | tf_op jit(solution)/shard_map/all_gather | solution.py:71
  397.6 5.4 %fusion.87 = (bf16[384,1024]{0,1:T(8,128)(2,1)}, bf16[384,1024]{0,1:T(8,128)(2,1)}, bf16[384,1024]{0,1:T(8,128)(2,1)}, bf16[384,1024]{0,1:T(8,128)(2,1)}, bf16[3...) fusion(bf16[3072,1024]{0,1:T(8,128)(2,1)} %all-gather.26.cloned., ...), kind=kLoop, calls=%fused_computation.137 | loop fusion | bytes 12582912 | tf_op jit(solution)/shard_map/slice | solution.py:76
  404.3 36.4 %all-gather.28.cloned.1.call-done = bf16[3072,1024]{0,1:T(8,128)(2,1)} async-done(((bf16[384,1024]{0,1:T(8,128)(2,1)}), bf16[3072,1024]{0,1:T(8,128)(2,1)}) %all-gather.28.cloned.1.call-update) | async-done | bytes 6291472 | tf_op jit(solution)/shard_map/all_gather | solution.py:71
  440.7 2.8 fusion.60
  459.6 12.4 %add_convert_fusion = bf16[12,768,2,128]{1,3,2,0:T(8,128)(2,1)S(1)} fusion(f32[2,128]{1,0:T(2,128)S(1)} %convert_element_type.171, bf16[12,768,1024]{1,2,0:T(8,128)(2,1)} %fusion.68, bf16[2,1024,128]{2,1,0:T(8,128)(2,1)S(1)} %copy-done), kind=kOutput, calls=%fused_computation.31 | convolution fusion | flops 4836556800 | bytes 24118272 | tf_op jit(solution)/shard_map/bfd,ldc->lbfc/dot_general | solution.py:81
  474.6 6.7 %fusion.42 = bf16[12,768,2,128]{1,3,2,0:T(8,128)(2,1)S(1)} fusion(bf16[12,768,1024]{1,2,0:T(8,128)(2,1)S(1)} %bitcast.183, bf16[2,1024,128]{2,1,0:T(8,128)(2,1)} %param.39), kind=kOutput, calls=%fused_computation.69 | convolution fusion | flops 4834197504 | bytes 24117248 | tf_op jit(solution)/shard_map/bfd,ldc->lbfc/dot_general | solution.py:80
  486.5 4.5 copy.146
  (168 shorter events, 74.6 us)
Async XLA Ops:
  7.2 452.4 %copy-start = (bf16[2,1024,128]{2,1,0:T(8,128)(2,1)S(1)}, bf16[2,1024,128]{2,1,0:T(8,128)(2,1)}, u32[]{:S(2)}) copy-start(bf16[2,1024,128]{2,1,0:T(8,128)(2,1)} %param.40) | copy-start | bytes 1572868
  7.2 118.3 %all-gather.20.cloned.1.call-start = ((), (), s32[]{:S(2)}) async-start(), calls=%async_computation.3 | async-start | bytes 7077888 | tf_op jit(solution)/shard_map/all_gather | solution.py:33
  9.5 213.1 %all-gather.16.cloned.1.call-start = ((), (), s32[]{:S(2)}) async-start(), calls=%async_computation.1 | async-start | bytes 2359296 | tf_op jit(solution)/shard_map/all_gather | solution.py:34
  10.3 219.2 %all-gather.22.cloned.1.call-start = ((), (), s32[]{:S(2)}) async-start(), calls=%async_computation.4 | async-start | bytes 9437184 | tf_op jit(solution)/shard_map/all_gather | solution.py:35
  12.3 6.8 %copy-start.31 = (bf16[128]{0:T(256)(128)(2,1)S(1)}, bf16[128]{0:T(256)(128)(2,1)}, u32[]{:S(2)}) copy-start(bf16[128]{0:T(256)(128)(2,1)} %param.25) | copy-start | bytes 772
  12.3 59.9 %copy-start.32 = (bf16[128]{0:T(256)(128)(2,1)S(1)}, bf16[128]{0:T(256)(128)(2,1)}, u32[]{:S(2)}) copy-start(bf16[128]{0:T(256)(128)(2,1)} %param.28) | copy-start | bytes 772
  12.3 70.7 %copy-start.24 = (bf16[1024]{0:T(1024)(128)(2,1)S(1)}, bf16[1024]{0:T(1024)(128)(2,1)}, u32[]{:S(2)}) copy-start(bf16[1024]{0:T(1024)(128)(2,1)} %param.30) | copy-start | bytes 6148
  12.3 70.7 %copy-start.25 = (bf16[1024]{0:T(1024)(128)(2,1)S(1)}, bf16[1024]{0:T(1024)(128)(2,1)}, u32[]{:S(2)}) copy-start(bf16[1024]{0:T(1024)(128)(2,1)} %param.31) | copy-start | bytes 6148
  12.3 70.7 %copy-start.26 = (bf16[1024]{0:T(1024)(128)(2,1)S(1)}, bf16[1024]{0:T(1024)(128)(2,1)}, u32[]{:S(2)}) copy-start(bf16[1024]{0:T(1024)(128)(2,1)} %param.32) | copy-start | bytes 6148
  12.3 70.7 %copy-start.30 = (bf16[512]{0:T(512)(128)(2,1)S(1)}, bf16[512]{0:T(512)(128)(2,1)}, u32[]{:S(2)}) copy-start(bf16[512]{0:T(512)(128)(2,1)} %param.34) | copy-start | bytes 3076
  12.3 82.1 %copy-start.27 = (bf16[1024]{0:T(1024)(128)(2,1)S(1)}, bf16[1024]{0:T(1024)(128)(2,1)}, u32[]{:S(2)}) copy-start(bf16[1024]{0:T(1024)(128)(2,1)} %param.36) | copy-start | bytes 6148
  12.4 82.7 %copy-start.28 = (bf16[1024]{0:T(1024)(128)(2,1)S(1)}, bf16[1024]{0:T(1024)(128)(2,1)}, u32[]{:S(2)}) copy-start(bf16[1024]{0:T(1024)(128)(2,1)} %param.37) | copy-start | bytes 6148
  12.4 83.3 %copy-start.29 = (bf16[1024]{0:T(1024)(128)(2,1)S(1)}, bf16[1024]{0:T(1024)(128)(2,1)}, u32[]{:S(2)}) copy-start(bf16[1024]{0:T(1024)(128)(2,1)} %param.38) | copy-start | bytes 6148
  14.1 82.1 %all-to-all-start = ((bf16[8,2,96,1024]{3,2,1,0:T(8,128)(2,1)}), bf16[8,2,96,1024]{3,2,1,0:T(8,128)(2,1)}, u32[]{:S(2)}, u32[]{:S(2)}) async-start(bf16[8,2,96,1024]{3,2,1,0:T(8,128)(2,1)} %bitcast.167), calls=%async_computation | async-start | bytes 6291456 | tf_op jit(solution)/shard_map/all_to_all | solution.py:28
  18.5 275.4 %all-gather.18.cloned.1.call-start = ((), (), s32[]{:S(2)}) async-start(), calls=%async_computation.2 | async-start | bytes 9437184 | tf_op jit(solution)/shard_map/all_gather | solution.py:36
  19.0 335.5 %all-gather.24.cloned.1.call-start = ((), (), s32[]{:S(2)}) async-start(), calls=%async_computation.5 | async-start | bytes 7077888 | tf_op jit(solution)/shard_map/all_gather | solution.py:71
  176.1 11.0 %copy-start.15 = (bf16[768,16,64]{0,2,1:T(8,128)(2,1)S(1)}, bf16[768,16,64]{0,2,1:T(8,128)(2,1)}, u32[]{:S(2)}) copy-start(bf16[768,16,64]{0,2,1:T(8,128)(2,1)} %reshape.130) | copy-start | bytes 4718596
  187.1 16.0 %copy-start.17 = (bf16[1,384,1024]{1,2,0:T(8,128)(2,1)S(1)}, bf16[1,384,1024]{1,2,0:T(8,128)(2,1)}, u32[]{:S(2)}) copy-start(bf16[1,384,1024]{1,2,0:T(8,128)(2,1)} %copy.139) | copy-start | bytes 2359300
  203.2 7.0 %copy-start.16 = (bf16[1,768,1024]{1,2,0:T(8,128)(2,1)S(1)}, bf16[1,768,1024]{1,2,0:T(8,128)(2,1)}, u32[]{:S(2)}) copy-start(bf16[1,768,1024]{1,2,0:T(8,128)(2,1)} %copy.138) | copy-start | bytes 4718596
  229.4 17.6 %copy-start.18 = (f32[8,1,512]{2,1,0:T(1,128)S(1)}, f32[8,1,512]{2,1,0:T(1,128)}, u32[]{:S(2)}) copy-start(f32[8,1,512]{2,1,0:T(1,128)} %convert_element_type.177) | copy-start | bytes 49156
  247.1 46.8 %copy-start.21 = (f32[1024]{0:T(1024)S(1)}, f32[1024]{0:T(1024)}, u32[]{:S(2)}) copy-start(f32[1024]{0:T(1024)} %convert_element_type.161) | copy-start | bytes 12292
  293.9 17.4 %copy-start.19 = (f32[1024]{0:T(1024)S(1)}, f32[1024]{0:T(1024)}, u32[]{:S(2)}) copy-start(f32[1024]{0:T(1024)} %convert_element_type.166) | copy-start | bytes 12292
  293.9 17.4 %copy-start.20 = (f32[1024]{0:T(1024)S(1)}, f32[1024]{0:T(1024)}, u32[]{:S(2)}) copy-start(f32[1024]{0:T(1024)} %convert_element_type.167) | copy-start | bytes 12292
  313.7 83.9 %all-gather.26.cloned.1.call-start = ((), (), s32[]{:S(2)}) async-start(), calls=%async_computation.6 | async-start | bytes 7077888 | tf_op jit(solution)/shard_map/all_gather | solution.py:71
  314.3 126.5 %all-gather.28.cloned.1.call-start = ((), (), s32[]{:S(2)}) async-start(), calls=%async_computation.7 | async-start | bytes 7077888 | tf_op jit(solution)/shard_map/all_gather | solution.py:71
  440.7 8.4 %copy-start.3 = (bf16[3072,1024]{0,1:T(8,128)(2,1)S(1)}, bf16[3072,1024]{0,1:T(8,128)(2,1)}, u32[]{:S(2)}) copy-start(bf16[3072,1024]{0,1:T(8,128)(2,1)} %all-gather.28.cloned.1.call-done) | copy-start | bytes 18874372
  443.5 6.9 %copy-start.8 = (bf16[384,1024]{0,1:T(8,128)(2,1)S(1)}, bf16[384,1024]{0,1:T(8,128)(2,1)}, u32[]{:S(2)}) copy-start(bf16[384,1024]{0,1:T(8,128)(2,1)} %get-tuple-element.25) | copy-start | bytes 2359300
  443.5 6.9 %copy-start.12 = (bf16[384,1024]{0,1:T(8,128)(2,1)S(1)}, bf16[384,1024]{0,1:T(8,128)(2,1)}, u32[]{:S(2)}) copy-start(bf16[384,1024]{0,1:T(8,128)(2,1)} %get-tuple-element.33) | copy-start | bytes 2359300
  459.6 15.0 %slice-start.1 = ((s8[18874368]{0:T(1024)(128)(4,1)}), s8[4194304]{0:T(1024)(128)(4,1)S(1)}, s32[]{:S(2)}) async-start(s8[18874368]{0:T(1024)(128)(4,1)} %bitcast.182), calls=%async_computation.9 | async-start | bytes 8388608
  459.6 15.0 %slice-start.2 = ((s8[18874368]{0:T(1024)(128)(4,1)}), s8[4194304]{0:T(1024)(128)(4,1)S(1)}, s32[]{:S(2)}) async-start(s8[18874368]{0:T(1024)(128)(4,1)} %bitcast.182), calls=%async_computation.10 | async-start | bytes 8388608
  459.6 15.0 %slice-start.3 = ((s8[18874368]{0:T(1024)(128)(4,1)}), s8[4194304]{0:T(1024)(128)(4,1)S(1)}, s32[]{:S(2)}) async-start(s8[18874368]{0:T(1024)(128)(4,1)} %bitcast.182), calls=%async_computation.11 | async-start | bytes 8388608
  459.6 15.0 %slice-start.4 = ((s8[18874368]{0:T(1024)(128)(4,1)}), s8[4194304]{0:T(1024)(128)(4,1)S(1)}, s32[]{:S(2)}) async-start(s8[18874368]{0:T(1024)(128)(4,1)} %bitcast.182), calls=%async_computation.12 | async-start | bytes 8388608
  (16 other events, 65.5 us)
Sparse Core Ops, SparseCore 0:
  9.8 71.9 all-gather.19
  83.6 21.7 all-gather.15
  107.2 48.3 all-gather.21
  157.2 48.3 all-gather.17
  313.8 40.7 all-gather.23
  356.8 40.7 all-gather.25
  399.9 40.7 all-gather.27
